TPU v7x, 32 devices: a whole 2x2x4 slice. The times are simulated.
32 devices in a mesh: seq: 16 (over z, y, core), dp: 2 (over x).
Axes of the slice: x: 2, y: 2, z: 4, core: 2. Of those that a mesh axis runs over, the one named last changes fastest.
Arguments:
- acceptors: bfloat16 [2, 2048, 2560], P('dp', 'seq'), may hold values from -2 to 2
- lookups: bfloat16 [2, 2048, 2560], P('dp', 'seq'), may hold values from -0.625 to 0.625
- payloads: bfloat16 [2, 2048, 2560], P('dp', 'seq'), may hold values from -6 to 6
- lagged_fading_source: bfloat16 [2, 2048, 2560], P('dp', 'seq'), may hold values from -6 to 6
- response_cotangent: bfloat16 [2, 2048, 2560], P('dp', 'seq'), may hold values from -5 to 5
- fading_lowering_array: bfloat16 [2560, 128], replicated, may hold values from -0.125 to 0.125
- fading_raising_array: bfloat16 [2560, 128], replicated, may hold values from -1.25 to 1.25
- feature_fading_speed: float32 [2560], replicated, may hold values from 2.3251488e-05 to 0.125
- present_reward: float32 [2560], replicated, may hold values from 1.4142135 to 11.313708
Outputs:
- mixed: bfloat16 [2, 2048, 2560], P('dp', 'seq')
- grad_receptance: bfloat16 [2, 2048, 2560], P('dp', 'seq')
- lookup_deriv: bfloat16 [2, 2048, 2560], P('dp', 'seq')
- payload_deriv: bfloat16 [2, 2048, 2560], P('dp', 'seq')
- grad_decay_input: bfloat16 [2, 2048, 2560], P('dp', 'seq')
- grad_lora_a: float32 [2560, 128], P('dp')
- grad_lora_b: float32 [2560, 128], P('dp')
- grad_time_decay: float32 [2560], P('dp')
- present_reward_deriv: float32 [2560], P('dp')
All inputs are finite; a program needn't handle non-finite values.
Results may differ from a plain program's by a relative error of at most 0.006.
Values sent between devices are 32-bit elements.
A program may use at most 320 MiB of HBM per device.

v0:
```python
import jax
import jax.numpy as jnp
from jax import lax
from jax.sharding import PartitionSpec as P

ATTENDER_TOTAL = 40
LANE_TOTAL = 64
BLOCK = 64
HIGH = lax.Precision.HIGHEST


def carried_in(part, axis, combine, identity, reverse):
    count = lax.axis_size(axis)
    place = lax.axis_index(axis)
    ahead = count - 1 - place if reverse else place
    gathered = jax.tree.map(lambda a: lax.all_gather(a, axis), part)
    state = jax.tree.map(lambda a, e: jnp.zeros_like(a) + jnp.asarray(e, a.dtype), part, identity)

    def one(hop, state):
        source = count - 1 - hop if reverse else hop
        return combine(
            state, jax.tree.map(lambda a: lax.dynamic_index_in_dim(a, source, 0, False), gathered)
        )

    return lax.fori_loop(0, ahead, one, state)


def contract(pattern, left, right):
    return jnp.einsum(pattern, left, right, precision=HIGH, preferred_element_type=jnp.float32)


def decay_log_values(input_rows, fading_lowering_array, fading_raising_array, feature_fading_speed):
    apply_projection = jnp.dot(
        input_rows, fading_lowering_array, preferred_element_type=jnp.float32
    )
    smoothed_values = jnp.tanh(apply_projection)
    gate_portion = smoothed_values.astype(jnp.bfloat16)
    rank_projection = lax.dot_general(
        gate_portion,
        fading_raising_array,
        (((1,), (1,)), ((), ())),
        preferred_element_type=jnp.float32,
    )
    return (
        smoothed_values,
        gate_portion,
        -feature_fading_speed[None, :] * jnp.exp(rank_projection),
    )


def compose(decays, own_states, backward):

    def advance(carry, member):
        run_decay, run_state = carry
        decay, own_state = member
        return ((run_decay * decay, decay[..., None] * run_state + own_state), carry)

    initial = (
        jnp.ones(decays.shape[1:], jnp.float32),
        jnp.zeros(own_states.shape[1:], jnp.float32),
    )
    return lax.scan(advance, initial, (decays, own_states), reverse=backward)


def follow(earlier, later):
    return (earlier[0] * later[0], later[0][..., None] * earlier[1] + later[1])


def temporal_blend_sublevel(
    acceptor_lines,
    lookups,
    payloads,
    incoming_cotangent,
    fading_exponent,
    reward_by_attender,
    adjacent_shardlink,
):
    inclusive = jnp.cumsum(fading_exponent, axis=1)
    exclusive = inclusive - fading_exponent
    middle = inclusive[:, BLOCK // 2 - 1 : BLOCK // 2]
    overall = inclusive[:, -1]
    entering = jnp.exp(exclusive)
    leaving = jnp.exp(overall[:, None] - inclusive)
    upward = jnp.exp(exclusive - middle)
    downward = jnp.exp(middle - inclusive)
    decays = jnp.exp(overall)
    reached = acceptor_lines * entering
    faded_keys = lookups * leaving
    own_states = contract("nchk,nchv->nhkv", faded_keys, payloads)
    pull_states = contract("nchk,nchv->nhkv", reached, incoming_cotangent)
    starts, block_ends = adjacent_shardlink(decays, own_states, pull_states)
    position = jnp.arange(BLOCK)
    beneath = position[:, None] > position[None, :]
    early_recept = acceptor_lines * upward
    late_keys = lookups * downward
    scores = jnp.where(beneath, contract("nthk,nshk->nhts", early_recept, late_keys), 0.0)
    present_contribution = jnp.sum(acceptor_lines * reward_by_attender * lookups, axis=-1)[
        ..., None
    ]
    blended_response = (
        contract("nhts,nshv->nthv", scores, payloads)
        + present_contribution * payloads
        + contract("nthk,nhkv->nthv", reached, starts)
    )
    grad_start = decays[..., None] * block_ends + pull_states
    products = jnp.where(beneath, contract("nthv,nshv->nhts", incoming_cotangent, payloads), 0.0)
    agreement_verify = jnp.sum(payloads * incoming_cotangent, axis=-1)[..., None]
    memory_acceptors = entering * contract(
        "nhkv,nthv->nthk", starts, incoming_cotangent
    ) + upward * contract("nhts,nshk->nthk", products, late_keys)
    memory_lookup_lines = leaving * contract(
        "nhkv,nthv->nthk", block_ends, payloads
    ) + downward * contract("nhst,nshk->nthk", products, early_recept)
    payload_deriv = (
        contract("nthk,nhkv->nthv", faded_keys, block_ends)
        + contract("nhst,nshv->nthv", scores, incoming_cotangent)
        + present_contribution * incoming_cotangent
    )
    acceptor_deriv = memory_acceptors + reward_by_attender * lookups * agreement_verify
    lookup_deriv = memory_lookup_lines + reward_by_attender * acceptor_lines * agreement_verify
    present_reward_deriv = jnp.sum(acceptor_lines * lookups * agreement_verify, axis=(0, 1))
    coupling = jnp.sum(grad_start * starts, axis=-1)
    change = lookups * memory_lookup_lines - acceptor_lines * memory_acceptors
    fading_deriv = (
        coupling[:, None] + jnp.cumsum(change, axis=1) - change - acceptor_lines * memory_acceptors
    )
    return (
        blended_response,
        acceptor_deriv,
        lookup_deriv,
        payload_deriv,
        fading_deriv,
        present_reward_deriv,
    )


def sublevel_evaluation(
    reshaped_acceptors,
    reshaped_lookups,
    reshaped_payloads,
    reshaped_source,
    incoming_cotangent_reshaped,
    fading_lowering_array,
    fading_raising_array,
    feature_fading_speed,
    present_reward,
    adjacent_shardlink,
):
    smoothed_values, gate_portion, fading_exponent = decay_log_values(
        reshaped_source, fading_lowering_array, fading_raising_array, feature_fading_speed
    )
    tokens, feature_span = reshaped_acceptors.shape
    tiling_arrangement = (tokens // BLOCK, BLOCK, ATTENDER_TOTAL, LANE_TOTAL)
    collected_outcomes = temporal_blend_sublevel(
        reshaped_acceptors.astype(jnp.float32).reshape(tiling_arrangement),
        reshaped_lookups.astype(jnp.float32).reshape(tiling_arrangement),
        reshaped_payloads.astype(jnp.float32).reshape(tiling_arrangement),
        incoming_cotangent_reshaped.astype(jnp.float32).reshape(tiling_arrangement),
        fading_exponent.reshape(tiling_arrangement),
        present_reward.reshape(ATTENDER_TOTAL, LANE_TOTAL),
        adjacent_shardlink,
    )
    (
        blended_response,
        acceptor_deriv,
        lookup_deriv,
        payload_deriv,
        fading_deriv,
        present_reward_deriv,
    ) = collected_outcomes
    slope = fading_deriv.reshape(tokens, feature_span) * fading_exponent
    slope_portion = slope.astype(jnp.bfloat16)
    gate_gradient = jnp.dot(slope_portion, fading_raising_array, preferred_element_type=jnp.float32)
    projection_gradient = (gate_gradient * (1.0 - smoothed_values * smoothed_values)).astype(
        jnp.bfloat16
    )
    input_gradient = lax.dot_general(
        projection_gradient,
        fading_lowering_array,
        (((1,), (1,)), ((), ())),
        preferred_element_type=jnp.float32,
    ).astype(jnp.bfloat16)
    lowering_array_deriv = lax.dot_general(
        reshaped_source,
        projection_gradient,
        (((0,), (0,)), ((), ())),
        preferred_element_type=jnp.float32,
    )
    raising_array_deriv = lax.dot_general(
        slope_portion, gate_portion, (((0,), (0,)), ((), ())), preferred_element_type=jnp.float32
    )
    speed_deriv = jnp.sum(slope, axis=0)

    def flatten(member):
        return member.reshape(tokens, feature_span).astype(jnp.bfloat16)

    return (
        flatten(blended_response),
        flatten(acceptor_deriv),
        flatten(lookup_deriv),
        flatten(payload_deriv),
        input_gradient,
        (
            lowering_array_deriv,
            raising_array_deriv,
            speed_deriv,
            present_reward_deriv.reshape(feature_span),
        ),
    )


def shard_link(decays, own_states, pull_states):
    ahead_total, ahead = compose(decays, own_states, False)
    behind_total, behind = compose(decays, pull_states, True)
    identity = (jnp.ones_like(ahead_total[0]), jnp.zeros_like(ahead_total[1]))
    prior, state_in = carried_in(ahead_total, "seq", follow, identity, False)
    latter, grad_after = carried_in(behind_total, "seq", follow, identity, True)
    starts = ahead[0][..., None] * state_in[None] + ahead[1]
    block_ends = behind[0][..., None] * grad_after[None] + behind[1]
    return (starts, block_ends)


def per_device(
    acceptors,
    lookups,
    payloads,
    lagged_fading_source,
    response_cotangent,
    fading_lowering_array,
    fading_raising_array,
    feature_fading_speed,
    present_reward,
):
    collected_outcomes = sublevel_evaluation(
        acceptors[0],
        lookups[0],
        payloads[0],
        lagged_fading_source[0],
        response_cotangent[0],
        fading_lowering_array,
        fading_raising_array,
        feature_fading_speed,
        present_reward,
        shard_link,
    )
    sums = collected_outcomes[5]
    dp_count = lax.axis_size("dp")
    share_rows = fading_lowering_array.shape[0] // dp_count
    whole = lax.psum((sums[0], sums[1], sums[2], sums[3]), ("seq", "dp"))
    offset = lax.axis_index("dp") * share_rows
    reduced = tuple((lax.dynamic_slice_in_dim(member, offset, share_rows, 0) for member in whole))
    return (
        collected_outcomes[0][None],
        collected_outcomes[1][None],
        collected_outcomes[2][None],
        collected_outcomes[3][None],
        collected_outcomes[4][None],
        reduced[0],
        reduced[1],
        reduced[2],
        reduced[3],
    )


def solution(mesh):
    in_specs = (
        P("dp", "seq", None),
        P("dp", "seq", None),
        P("dp", "seq", None),
        P("dp", "seq", None),
        P("dp", "seq", None),
        P(),
        P(),
        P(),
        P(),
    )
    out_specs = (
        P("dp", "seq", None),
        P("dp", "seq", None),
        P("dp", "seq", None),
        P("dp", "seq", None),
        P("dp", "seq", None),
        P("dp", None),
        P("dp", None),
        P("dp"),
        P("dp"),
    )
    return jax.shard_map(
        per_device, mesh=mesh, in_specs=in_specs, out_specs=out_specs, check_vma=False
    )
```

profile of v0, /device:TPU:0, one launch (start us, length us, event | category | flops | bytes accessed | tf_op | source)
XLA Modules:
  0.0 555.1 jit_solution(3904437213683768561)
XLA Ops:
  19.8 2.9 reshape.128
  22.7 3.2 copy.93
  28.6 5.5 fusion.57
  36.0 17.7 %while.66 = (s32[]{:T(128)}, f32[40,64]{1,0:T(8,128)S(1)}, f32[40,64,64]{2,1,0:T(8,128)}, f32[2,40,64]{2,1,0:T(8,128)S(1)}, f32[2,40,64,64]{2,3,1,0:T(8,128)}, /...) while((s32[]{:T(128)}, f32[40,64]{1,0:T(8,128)S(1)}, ...), condition=%wide.region_3.4_spmd.clone, body=%wide.region_2.3_spmd.clone.sunk | while | flops 499203 | bytes 6646389 | solution.py:62
  36.0 3.2 select_bitcast_fusion.4
  39.3 2.8 copy.180
  44.6 3.6 select_bitcast_fusion.4
  48.3 2.8 copy.180
  53.9 3.3 copy.90
  59.8 2.8 reshape.127
  62.6 3.6 copy.91
  66.2 7.1 %fusion.50 = f32[2,40,64,64]{2,3,1,0:T(8,128)} fusion(f32[2,64,40,64]{1,3,2,0:T(8,128)} %copy.91, bf16[2,64,40,64]{3,2,1,0:T(8,128)(2,1)} %reshape.125, f32[2,64,40,64]{1,3,2,0:T(8,128)S(1)} %copy.89, f32[2,64,40,64]{1,3,2,0:T(8,128)} %copy.90), kind=kOutput, calls=%fused_computation.85 | convolution fusion | flops 252313600 | bytes 5898240 | tf_op jit(solution)/shard_map/nchk,nchv->nhkv/dot_general | solution.py:29
  75.7 29.7 %while.67 = (s32[]{:T(128)}, f32[40,64]{1,0:T(8,128)S(1)}, f32[40,64,64]{2,1,0:T(8,128)}, f32[2,40,64]{2,1,0:T(8,128)}, f32[2,40,64,64]{2,3,1,0:T(8,128)}, /*ind...) while((s32[]{:T(128)}, f32[40,64]{1,0:T(8,128)S(1)}, ...), condition=%wide.region_8.9_spmd.clone, body=%wide.region_7.8_spmd.clone.sunk | while | flops 499204 | bytes 9257093 | solution.py:62
  76.3 2.7 constant_dynamic-slice_fusion.4
  79.0 2.8 copy.181
  81.8 3.3 select_bitcast_fusion.5
  85.0 2.8 copy.182
  93.6 2.8 copy.181
  96.4 3.7 select_bitcast_fusion.5
  100.1 2.8 copy.182
  106.3 3.1 fusion.5
  110.8 2.7 mul.266.clone
  113.5 2.9 mul.285
  116.3 27.7 %all-gather = f32[640,64]{1,0:T(8,128)} all-gather(f32[40,64]{1,0:T(8,128)S(1)} %get-tuple-element.322), channel_id=2, replica_groups=mesh['seq'=16,'dp'=2] {'seq'}, dimensions={0}, use_global_device_ids=true | all-gather | bytes 174080 | tf_op jit(solution)/shard_map/all_gather | solution.py:16
  144.0 21.9 %all-gather.2 = f32[640,64]{1,0:T(8,128)} all-gather(f32[40,64]{1,0:T(8,128)S(1)} %get-tuple-element.327), channel_id=4, replica_groups=mesh['seq'=16,'dp'=2] {'seq'}, dimensions={0}, use_global_device_ids=true | all-gather | bytes 174080 | tf_op jit(solution)/shard_map/all_gather | solution.py:16
  166.0 2.8 multiply_reduce_fusion.2
  168.8 4.1 fusion.62
  172.9 7.7 %fusion.52 = f32[2,40,64,64]{3,2,1,0:T(8,128)} fusion(f32[2,64,40,64]{1,3,2,0:T(8,128)S(1)} %copy-done.3, f32[2,64,40,64]{1,3,2,0:T(8,128)S(1)} %copy.89, f32[2,40,64]{2,1,0:T(8,128)S(1)} %get-tuple-element.494, f32[2,64,40,64]{1,3,2,0:T(8,128)S(1)} %copy-done.6, f32[2,64,40,64]{1,3,2,0:T(8,128)S(1)} %copy-done.1), kind=kOutput, calls=%fused_computation.86 | convolution fusion | flops 253296640 | bytes 6574080 | tf_op jit(solution)/shard_map/nthk,nshk->nhts/dot_general | solution.py:29
  182.0 2.8 copy.103
  184.8 97.0 %all-gather.9.cloned.1.call-done = f32[640,64,64]{2,1,0:T(8,128)} async-done(((f32[40,64,64]{2,1,0:T(8,128)}), f32[640,64,64]{2,1,0:T(8,128)}) %all-gather.9.cloned.1.call-update) | async-done | bytes 10485776 | tf_op jit(solution)/shard_map/all_gather | solution.py:16
  283.1 60.2 %while.65 = (s32[]{:T(128)}, f32[40,64,64]{2,1,0:T(8,128)}, s32[]{:T(128)}, f32[16,40,64]{2,1,0:T(8,128)}, f32[16,40,64,64]{3,2,1,0:T(8,128)}, /*index=5*/s32[]{:T(128)}, s32[]{:T(128)}, s32[]{:T(128)}, s32[]{:T(128)}) while((s32[]{:T(128)}, f32[40,64,64]{2,1,0:T(8,128)}, s32[]{:T(128)}, f32[16,40,64]{2,1,0:T(8,128)}, ...), condition=%wide.region_10.11_spmd, body=%wide.region_9.10_spmd.sunk | while | flops 327686 | bytes 1996947 | solution.py:25
  283.8 3.3 bitcast_add_fusion.8
  287.8 3.3 bitcast_add_fusion.8
  291.8 3.3 bitcast_add_fusion.8
  295.8 3.3 bitcast_add_fusion.8
  299.8 3.3 bitcast_add_fusion.8
  303.9 3.3 bitcast_add_fusion.8
  307.9 3.3 bitcast_add_fusion.8
  311.9 3.3 bitcast_add_fusion.8
  315.9 3.3 bitcast_add_fusion.8
  319.9 3.3 bitcast_add_fusion.8
  323.9 3.3 bitcast_add_fusion.8
  327.9 3.3 bitcast_add_fusion.8
  331.9 3.3 bitcast_add_fusion.8
  335.9 3.3 bitcast_add_fusion.8
  339.9 3.3 bitcast_add_fusion.8
  343.2 2.8 copy.119
  346.1 6.4 %fusion.24 = f32[2,40,64,64]{3,2,1,0:T(8,128)} fusion(f32[2,40,64,64]{2,3,1,0:T(8,128)} %get-tuple-element.330, f32[40,64,64]{1,2,0:T(8,128)} %copy.119, f32[2,40,64]{2,1,0:T(8,128)S(1)} %copy-done.23, bf16[2,64,40,64]{3,2,1,0:T(8,128)(2,1)} %reshape.124), kind=kOutput, calls=%fused_computation.64 | convolution fusion | flops 252313600 | bytes 3952640 | tf_op jit(solution)/shard_map/nhkv,nthv->nthk/dot_general | solution.py:29
  352.5 4.1 multiply_reduce_fusion
  359.9 6.5 %fusion.9 = f32[2,64,40,64]{1,3,2,0:T(8,128)} fusion(f32[2,40,64,64]{3,2,1,0:T(8,128)S(1)} %fusion.21, f32[2,40,64,64]{3,2,1,0:T(8,128)S(1)} %copy-done.16, f32[2,40,64]{2,1,0:T(8,128)S(1)} %get-tuple-element.494, pred[64,64]{1,0:T(8,128)(4,1)S(1)} %iota_compare_fusion, f32[2,64,40,64]{1,3,2,0:T(8,128)S(1)} %copy-done.4, f32[2,64,40,64]{1,3,2,0:T(8,128)S(1)} %copy.89, ...), kind=kOutput, calls=%fused_computation.36 | convolution fusion | flops 254279680 | bytes 7888896 | tf_op jit(solution)/shard_map/nhts,nshk->nthk/dot_general | solution.py:29
  366.4 11.1 %multiply_subtract_fusion = (f32[2,64,40,64]{1,3,2,0:T(8,128)}, f32[2,64,40,64]{1,3,2,0:T(8,128)}, bf16[2,64,40,64]{1,3,2,0:T(8,128)(2,1)}, bf16[2,64,40,64]{1,3,2,0:T(8,128)(2,1)}, f32[2,64,40]{1,2,0:T(8,128)}) fusion(f32[2,64,40,64]{1,3,2,0:T(8,128)S(1)} %copy-done.4, f32[2,64,40,64]{1,3,2,0:T(8,128)S(1)} %copy-done.7, f32[2,64,40,64]{1,3,2,0:T(8,128)} %fusion.9, ...), kind=kOutput, calls=%fused_computation.39 | convolution fusion | flops 258862080 | bytes 13203456 | tf_op jit(solution)/shard_map/nhst,nshk->nthk/dot_general | solution.py:29
  377.5 3.2 copy.131
  380.7 3.5 fusion.83
  384.2 3.2 copy.132
  387.4 5.0 subtract_subtract_fusion
  392.4 3.3 copy.133
  395.7 3.2 reshape.126
  403.0 6.6 %fusion.23 = f32[2,40,64,64]{2,3,1,0:T(8,128)} fusion(f32[2,40,64,64]{2,3,1,0:T(8,128)S(1)} %copy-done.13, f32[40,64,64]{1,2,0:T(8,128)S(1)} %copy-done.18, f32[2,40,64]{2,1,0:T(8,128)S(1)} %copy-done.24, f32[2,64,40,64]{1,3,2,0:T(8,128)S(1)} %copy-done.5, f32[2,64,40,64]{1,3,2,0:T(8,128)S(1)} %copy.89, f32[2,40,64]{2,1,0:T(8,128)S(1)} %copy-done.22), kind=kOutput, calls=%fused_computation.63 | convolution fusion | flops 252968960 | bytes 5939200 | tf_op jit(solution)/shard_map/nthk,nhkv->nthv/dot_general | solution.py:29
  411.1 7.4 %fusion.7 = bf16[2,64,40,64]{3,1,2,0:T(8,128)(2,1)} fusion(f32[2,40,64,64]{2,3,1,0:T(8,128)} %fusion.23, f32[2,40,64,64]{3,2,1,0:T(8,128)} %fusion.52, f32[2,64,40]{1,2,0:T(8,128)S(1)} %copy-done.26, pred[64,64]{1,0:T(8,128)(4,1)S(1)} %iota_compare_fusion, bf16[2,64,40,64]{3,2,1,0:T(8,128)(2,1)} %reshape.125), kind=kOutput, calls=%fused_computation.30 | convolution fusion | flops 253624320 | bytes 3956736 | tf_op jit(solution)/shard_map/nhst,nshv->nthv/dot_general | solution.py:29
  418.6 37.4 %all-reduce = (f32[2560]{0:T(1024)S(1)}, f32[2560]{0:T(1024)S(1)}) all-reduce(f32[2560]{0:T(1024)S(1)} %get-tuple-element.492, f32[2560]{0:T(1024)S(1)} %copy-done.29), channel_id=1, replica_groups=mesh['seq'=16,'dp'=2] {'seq','dp'}, use_global_device_ids=true, to_apply=%region_16.17 | all-reduce | flops 5120 | bytes 40960 | tf_op jit(solution)/shard_map/psum | solution.py:249
  457.3 3.2 copy.128
  460.6 2.8 convert_element_type.122
  463.3 8.7 %fusion.22 = f32[2,40,64,64]{2,3,1,0:T(8,128)S(1)} fusion(f32[2,40,64,64]{2,3,1,0:T(8,128)} %get-tuple-element.325, f32[40,64,64]{1,2,0:T(8,128)} %copy.103, f32[2,40,64]{2,1,0:T(8,128)S(1)} %get-tuple-element.321, f32[2,64,40,64]{1,3,2,0:T(8,128)} %copy.91, f32[2,64,40,64]{1,3,2,0:T(8,128)S(1)} %copy.89, f32[2,64,40,64]{1,3,2,0:T(8,128)} %copy.90), kind=kOutput, calls=%fused_computation.62 | convolution fusion | flops 252968960 | bytes 7229440 | tf_op jit(solution)/shard_map/nthk,nhkv->nthv/dot_general | solution.py:29
  485.3 59.9 %all-reduce.4.cloned.1.call-done = (f32[2560,128]{0,1:T(8,128)}, f32[2560,128]{1,0:T(8,128)}) async-done(((f32[2560,128]{0,1:T(8,128)}, f32[2560,128]{1,0:T(8,128)}), (f32[2560,128]{0,1:T(8,128)}, f32[2560,128]{1,0:T(8,128)})) %all-reduce.4.cloned.1.call-update) | async-done | bytes 2621456 | tf_op jit(solution)/shard_map/psum | solution.py:249
  (137 shorter events, 78.9 us)
Async XLA Ops:
  7.2 2.4 copy-start
  7.2 173.4 %all-gather.7.cloned.1.call-start = ((), (), s32[]{:S(2)}) async-start(), calls=%async_computation | async-start | bytes 22282240 | tf_op jit(solution)/shard_map/all_gather | solution.py:16
  12.8 1.5 copy-start.14
  18.9 9.7 %copy-start.21 = (f32[2,40,64]{2,1,0:T(8,128)}, f32[2,40,64]{2,1,0:T(8,128)S(1)}, u32[]{:S(2)}) copy-start(f32[2,40,64]{2,1,0:T(8,128)S(1)} %get-tuple-element.495) | copy-start | bytes 61444
  53.7 228.2 %all-gather.9.cloned.1.call-start = ((), (), s32[]{:S(2)}) async-start(), calls=%async_computation.1 | async-start | bytes 22282240 | tf_op jit(solution)/shard_map/all_gather | solution.py:16
  105.4 439.8 %all-reduce.4.cloned.1.call-start = ((), (), s32[]{:S(2)}) async-start(), calls=%async_computation.2 | async-start | bytes 5242880 | tf_op jit(solution)/shard_map/psum | solution.py:249
  166.0 6.9 %copy-start.6 = (f32[2,64,40,64]{1,3,2,0:T(8,128)S(1)}, f32[2,64,40,64]{1,3,2,0:T(8,128)}, u32[]{:S(2)}) copy-start(f32[2,64,40,64]{1,3,2,0:T(8,128)} %copy.91) | copy-start | bytes 3932164
  168.8 4.1 copy-start.1
  168.8 4.1 copy-start.3
  343.2 2.8 copy-start.23
  346.0 6.4 %copy-start.8 = (f32[2,40,64,64]{2,3,1,0:T(8,128)S(1)}, f32[2,40,64,64]{2,3,1,0:T(8,128)}, u32[]{:S(2)}) copy-start(f32[2,40,64,64]{2,3,1,0:T(8,128)} %get-tuple-element.773) | copy-start | bytes 3932164
  346.0 6.4 %copy-start.11 = (f32[2,40,64,64]{2,3,1,0:T(8,128)S(1)}, f32[2,40,64,64]{2,3,1,0:T(8,128)}, u32[]{:S(2)}) copy-start(f32[2,40,64,64]{2,3,1,0:T(8,128)} %get-tuple-element.325) | copy-start | bytes 3932164
  346.0 6.4 %copy-start.12 = (f32[2,40,64,64]{2,3,1,0:T(8,128)S(1)}, f32[2,40,64,64]{2,3,1,0:T(8,128)}, u32[]{:S(2)}) copy-start(f32[2,40,64,64]{2,3,1,0:T(8,128)} %get-tuple-element.330) | copy-start | bytes 3932164
  352.5 4.1 copy-start.10
  352.5 4.1 copy-start.17
  356.6 2.4 copy-start.2
  356.6 2.5 copy-start.4
  356.6 3.3 copy-start.16
  359.9 6.5 %copy-start.7 = (f32[2,64,40,64]{1,3,2,0:T(8,128)S(1)}, f32[2,64,40,64]{1,3,2,0:T(8,128)}, u32[]{:S(2)}) copy-start(f32[2,64,40,64]{1,3,2,0:T(8,128)} %copy.91) | copy-start | bytes 3932164
  359.9 6.5 %copy-start.22 = (f32[2,40,64]{2,1,0:T(8,128)S(1)}, f32[2,40,64]{2,1,0:T(8,128)}, u32[]{:S(2)}) copy-start(f32[2,40,64]{2,1,0:T(8,128)} %copy-done.21) | copy-start | bytes 61444
  359.9 6.5 %copy-start.25 = (f32[2,64,40]{1,2,0:T(8,128)S(1)}, f32[2,64,40]{1,2,0:T(8,128)}, u32[]{:S(2)}) copy-start(f32[2,64,40]{1,2,0:T(8,128)} %fusion.5) | copy-start | bytes 61444
  384.2 3.2 copy-start.28
  398.9 3.9 copy-start.5
  398.9 3.9 copy-start.13
  398.9 4.1 copy-start.18
  398.9 4.1 copy-start.24
  403.0 6.6 %copy-start.20 = (bf16[1,128,2560]{2,1,0:T(8,128)(2,1)S(1)}, bf16[1,128,2560]{2,1,0:T(8,128)(2,1)}, u32[]{:S(2)}) copy-start(bf16[1,128,2560]{2,1,0:T(8,128)(2,1)} %param.20) | copy-start | bytes 1966084
  409.7 1.4 copy-start.26
  411.1 7.5 %copy-start.29 = (f32[2560]{0:T(1024)S(1)}, f32[2560]{0:T(1024)}, u32[]{:S(2)}) copy-start(f32[2560]{0:T(1024)} %multiply_reduce_fusion.2) | copy-start | bytes 30724
  463.3 8.7 %copy-start.9 = (bf16[2,64,40,64]{3,2,1,0:T(8,128)(2,1)S(1)}, bf16[2,64,40,64]{3,2,1,0:T(8,128)(2,1)}, u32[]{:S(2)}) copy-start(bf16[2,64,40,64]{3,2,1,0:T(8,128)(2,1)} %reshape.124) | copy-start | bytes 1966084
  463.3 8.7 %copy-start.15 = (f32[2,40,64,64]{3,2,1,0:T(8,128)S(1)}, f32[2,40,64,64]{3,2,1,0:T(8,128)}, u32[]{:S(2)}) copy-start(f32[2,40,64,64]{3,2,1,0:T(8,128)} %fusion.52) | copy-start | bytes 3932164
  476.9 3.6 copy-start.19
  545.2 2.3 copy-start.27
Sparse Core Ops, SparseCore 0:
  53.8 117.4 all-gather.6
  172.8 108.9 all-gather.8
  411.2 133.9 all-reduce.3
where the time goes:
time: 564 us; the launch traced here: 555 us
  waiting for transfers between devices  157 us (28%)
  local copies, waits for them, and re-layouts  125 us (22%)
  other arithmetic  87.2 us (15%)
  blocking collectives  87 us (15%)
  matrix products  84.5 us (15%)
  between operations  14.3 us (3%)
    all_gather x2, waiting for transfers between devices, carried_in(): gathered = jax.tree.map(lambda a: lax.all_gather(a, axis), part)  97 us
    dot_general x12, matrix products, contract(): jnp.einsum(pattern, left, right, precision=HIGH, preferred_element_type=j...  76 us
    psum x1, waiting for transfers between devices, per_device(): whole = lax.psum((sums[0], sums[1], sums[2], sums[3]), ('seq', 'dp'))  59.9 us
    all_gather x2, blocking collectives, carried_in(): gathered = jax.tree.map(lambda a: lax.all_gather(a, axis), part)  49.6 us
    add x15, other arithmetic, follow(): return (earlier[0] * later[0], later[0][..., None] * earlier[1] + later[1])  49.2 us
    psum x1, blocking collectives, per_device(): whole = lax.psum((sums[0], sums[1], sums[2], sums[3]), ('seq', 'dp'))  37.4 us
    dynamic_update_slice x8, local copies, waits for them, and re-layouts, compose(): return lax.scan(advance, initial, (decays, own_states), reverse=backward)  21.4 us
    convert_element_type x8, local copies, waits for them, and re-layouts, flatten(): return member.reshape(tokens, feature_span).astype(jnp.bfloat16)  14.5 us
  transfers between devices with their start and end apart: 3, of which 2 were waited for; matrix products, arithmetic and copies ran while one was open for 21% of the time, Pallas kernels for 0%

commit v1 on v0

--- a/solution.py
+++ b/solution.py
@@ -246,7 +246,7 @@
     sums = collected_outcomes[5]
     dp_count = lax.axis_size("dp")
     share_rows = fading_lowering_array.shape[0] // dp_count
-    whole = lax.psum((sums[0], sums[1], sums[2], sums[3]), ("seq", "dp"))
+    whole = lax.psum(lax.psum((sums[0], sums[1], sums[2], sums[3]), "seq"), "dp")
     offset = lax.axis_index("dp") * share_rows
     reduced = tuple((lax.dynamic_slice_in_dim(member, offset, share_rows, 0) for member in whole))
     return (

time: 564 us -> 649 us (1.15)
  waiting for transfers between devices: 157 us -> 207 us
  blocking collectives: 87 us -> 129 us
    psum x1 -> x2, blocking collectives: 37.4 us -> 78.8 us  [the longest x1 58.1 us: per_device(): lax.psum((sums[0], sums[1], sums[2], sums[3]), 'seq')]
    psum x1 -> x2, waiting for transfers between devices: 59.9 us -> 91 us  [the longest x1 91 us: per_device(): lax.psum((sums[0], sums[1], sums[2], sums[3]), 'seq')]
    all_gather x2, waiting for transfers between devices: 97 us -> 116 us  [carried_in(): gathered = jax.tree.map(lambda a: lax.all_gather(a, axis), part)]
  transfers between devices with their start and end apart: 3 -> 4, of which waited for: 2 -> 3; matrix products, arithmetic and copies ran while one was open for 21% -> 18% of each run, Pallas kernels for 0% -> 0%
where the time goes in v1:
time: 649 us; the launch traced here: 640 us
  waiting for transfers between devices  207 us (32%)
  blocking collectives  129 us (20%)
  local copies, waits for them, and re-layouts  122 us (19%)
  other arithmetic  86 us (13%)
  matrix products  81.6 us (13%)
  between operations  14.3 us (2%)
    all_gather x2, waiting for transfers between devices, carried_in(): gathered = jax.tree.map(lambda a: lax.all_gather(a, axis), part)  116 us
    psum x1, waiting for transfers between devices, per_device(): lax.psum((sums[0], sums[1], sums[2], sums[3]), 'seq')  91 us
    dot_general x12, matrix products, contract(): jnp.einsum(pattern, left, right, precision=HIGH, preferred_element_type=j...  73.1 us
    psum x1, blocking collectives, per_device(): lax.psum((sums[0], sums[1], sums[2], sums[3]), 'seq')  58.1 us
    all_gather x2, blocking collectives, carried_in(): gathered = jax.tree.map(lambda a: lax.all_gather(a, axis), part)  49.8 us
    add x15, other arithmetic, follow(): return (earlier[0] * later[0], later[0][..., None] * earlier[1] + later[1])  49.1 us
    dynamic_update_slice x8, local copies, waits for them, and re-layouts, compose(): return lax.scan(advance, initial, (decays, own_states), reverse=backward)  21.5 us
    psum x1, blocking collectives, per_device(): lax.psum(lax.psum((sums[0], sums[1], sums[2], sums[3]), 'seq'), 'dp')  20.6 us
  transfers between devices with their start and end apart: 4, of which 3 were waited for; matrix products, arithmetic and copies ran while one was open for 18% of the time, Pallas kernels for 0%

profile of v1, /device:TPU:0, one launch (start us, length us, event | category | flops | bytes accessed | tf_op | source)
XLA Modules:
  0.0 640.1 jit_solution(8597746479509713004)
XLA Ops:
  19.8 2.9 reshape.128
  22.7 3.2 copy.93
  26.0 2.6 reshape.124
  28.6 5.5 fusion.57
  35.9 17.7 %while.66 = (s32[]{:T(128)}, f32[40,64]{1,0:T(8,128)S(1)}, f32[40,64,64]{2,1,0:T(8,128)}, f32[2,40,64]{2,1,0:T(8,128)S(1)}, f32[2,40,64,64]{2,3,1,0:T(8,128)}, /...) while((s32[]{:T(128)}, f32[40,64]{1,0:T(8,128)S(1)}, ...), condition=%wide.region_3.4_spmd.clone, body=%wide.region_2.3_spmd.clone.sunk | while | flops 499203 | bytes 6646389 | solution.py:62
  36.0 3.2 select_bitcast_fusion.4
  39.2 2.9 copy.180
  44.6 3.6 select_bitcast_fusion.4
  48.2 2.9 copy.180
  53.9 3.3 copy.90
  57.2 2.7 reshape.125
  59.9 2.8 reshape.127
  62.7 3.5 copy.91
  66.2 7.0 %fusion.50 = f32[2,40,64,64]{2,3,1,0:T(8,128)} fusion(f32[2,64,40,64]{1,3,2,0:T(8,128)} %copy.91, bf16[2,64,40,64]{3,2,1,0:T(8,128)(2,1)} %reshape.125, f32[2,64,40,64]{1,3,2,0:T(8,128)S(1)} %copy.89, f32[2,64,40,64]{1,3,2,0:T(8,128)} %copy.90), kind=kOutput, calls=%fused_computation.85 | convolution fusion | flops 252313600 | bytes 5898240 | tf_op jit(solution)/shard_map/nchk,nchv->nhkv/dot_general | solution.py:29
  75.7 29.7 %while.67 = (s32[]{:T(128)}, f32[40,64]{1,0:T(8,128)S(1)}, f32[40,64,64]{2,1,0:T(8,128)}, f32[2,40,64]{2,1,0:T(8,128)}, f32[2,40,64,64]{2,3,1,0:T(8,128)}, /*ind...) while((s32[]{:T(128)}, f32[40,64]{1,0:T(8,128)S(1)}, ...), condition=%wide.region_8.9_spmd.clone, body=%wide.region_7.8_spmd.clone.sunk | while | flops 499204 | bytes 9257093 | solution.py:62
  76.3 2.7 constant_dynamic-slice_fusion.4
  78.9 2.8 copy.181
  81.7 3.2 select_bitcast_fusion.5
  85.0 2.8 copy.182
  93.5 2.8 copy.181
  96.3 3.6 select_bitcast_fusion.5
  99.9 2.8 copy.182
  106.2 27.9 %all-gather = f32[640,64]{1,0:T(8,128)} all-gather(f32[40,64]{1,0:T(8,128)S(1)} %get-tuple-element.322), channel_id=2, replica_groups=mesh['seq'=16,'dp'=2] {'seq'}, dimensions={0}, use_global_device_ids=true | all-gather | bytes 174080 | tf_op jit(solution)/shard_map/all_gather | solution.py:16
  134.1 21.9 %all-gather.2 = f32[640,64]{1,0:T(8,128)} all-gather(f32[40,64]{1,0:T(8,128)S(1)} %get-tuple-element.327), channel_id=4, replica_groups=mesh['seq'=16,'dp'=2] {'seq'}, dimensions={0}, use_global_device_ids=true | all-gather | bytes 174080 | tf_op jit(solution)/shard_map/all_gather | solution.py:16
  156.0 3.2 fusion.5
  161.6 9.6 %all-gather.7.cloned.1.call-done = f32[640,64,64]{2,1,0:T(8,128)} async-done(((f32[40,64,64]{2,1,0:T(8,128)}), f32[640,64,64]{2,1,0:T(8,128)}) %all-gather.7.cloned.1.call-update) | async-done | bytes 10485776 | tf_op jit(solution)/shard_map/all_gather | solution.py:16
  172.4 2.8 copy.103
  175.3 106.6 %all-gather.9.cloned.1.call-done = f32[640,64,64]{2,1,0:T(8,128)} async-done(((f32[40,64,64]{2,1,0:T(8,128)}), f32[640,64,64]{2,1,0:T(8,128)}) %all-gather.9.cloned.1.call-update) | async-done | bytes 10485776 | tf_op jit(solution)/shard_map/all_gather | solution.py:16
  283.1 60.2 %while.65 = (s32[]{:T(128)}, f32[40,64,64]{2,1,0:T(8,128)}, s32[]{:T(128)}, f32[16,40,64]{2,1,0:T(8,128)}, f32[16,40,64,64]{3,2,1,0:T(8,128)}, /*index=5*/s32[]{:T(128)}, s32[]{:T(128)}, s32[]{:T(128)}, s32[]{:T(128)}) while((s32[]{:T(128)}, f32[40,64,64]{2,1,0:T(8,128)}, s32[]{:T(128)}, f32[16,40,64]{2,1,0:T(8,128)}, ...), condition=%wide.region_10.11_spmd, body=%wide.region_9.10_spmd.sunk | while | flops 327686 | bytes 1996947 | solution.py:25
  283.8 3.3 bitcast_add_fusion.8
  287.8 3.3 bitcast_add_fusion.8
  291.8 3.3 bitcast_add_fusion.8
  295.8 3.3 bitcast_add_fusion.8
  299.8 3.3 bitcast_add_fusion.8
  303.8 3.3 bitcast_add_fusion.8
  307.8 3.3 bitcast_add_fusion.8
  311.8 3.3 bitcast_add_fusion.8
  315.8 3.3 bitcast_add_fusion.8
  319.8 3.3 bitcast_add_fusion.8
  323.8 3.3 bitcast_add_fusion.8
  327.8 3.3 bitcast_add_fusion.8
  331.8 3.3 bitcast_add_fusion.8
  335.8 3.3 bitcast_add_fusion.8
  339.8 3.3 bitcast_add_fusion.8
  343.3 2.8 copy.119
  346.1 6.4 %fusion.24 = f32[2,40,64,64]{3,2,1,0:T(8,128)} fusion(f32[2,40,64,64]{2,3,1,0:T(8,128)} %get-tuple-element.330, f32[40,64,64]{1,2,0:T(8,128)} %copy.119, f32[2,40,64]{2,1,0:T(8,128)S(1)} %copy-done.21, bf16[2,64,40,64]{3,2,1,0:T(8,128)(2,1)} %reshape.124), kind=kOutput, calls=%fused_computation.64 | convolution fusion | flops 252313600 | bytes 3952640 | tf_op jit(solution)/shard_map/nhkv,nthv->nthk/dot_general | solution.py:29
  352.6 4.1 multiply_reduce_fusion
  360.0 6.8 %fusion.9 = f32[2,64,40,64]{1,3,2,0:T(8,128)} fusion(f32[2,40,64,64]{3,2,1,0:T(8,128)S(1)} %fusion.21, f32[2,40,64,64]{3,2,1,0:T(8,128)S(1)} %copy-done.15, f32[2,40,64]{2,1,0:T(8,128)S(1)} %get-tuple-element.498, pred[64,64]{1,0:T(8,128)(4,1)S(1)} %iota_compare_fusion, f32[2,64,40,64]{1,3,2,0:T(8,128)S(1)} %copy-done.2, f32[2,64,40,64]{1,3,2,0:T(8,128)S(1)} %copy.89, ...), kind=kOutput, calls=%fused_computation.36 | convolution fusion | flops 254279680 | bytes 7888896 | tf_op jit(solution)/shard_map/nhts,nshk->nthk/dot_general | solution.py:29
  366.8 11.1 %multiply_subtract_fusion = (f32[2,64,40,64]{1,3,2,0:T(8,128)}, f32[2,64,40,64]{1,3,2,0:T(8,128)}, bf16[2,64,40,64]{1,3,2,0:T(8,128)(2,1)}, bf16[2,64,40,64]{1,3,2,0:T(8,128)(2,1)}, f32[2,64,40]{1,2,0:T(8,128)}) fusion(f32[2,64,40,64]{1,3,2,0:T(8,128)S(1)} %copy-done.2, f32[2,64,40,64]{1,3,2,0:T(8,128)S(1)} %copy-done.3, f32[2,64,40,64]{1,3,2,0:T(8,128)} %fusion.9, ...), kind=kOutput, calls=%fused_computation.39 | convolution fusion | flops 258862080 | bytes 13203456 | tf_op jit(solution)/shard_map/nhst,nshk->nthk/dot_general | solution.py:29
  377.8 3.3 copy.131
  381.1 3.4 fusion.83
  384.5 3.3 copy.132
  387.8 4.9 subtract_subtract_fusion
  392.7 3.2 copy.133
  395.9 2.9 reshape.126
  406.6 3.1 mul.285
  411.6 91.0 %all-reduce.7.cloned.1.call-done = (f32[2560,128]{0,1:T(8,128)}, f32[2560,128]{1,0:T(8,128)}) async-done(((f32[2560,128]{0,1:T(8,128)}, f32[2560,128]{1,0:T(8,128)}), (f32[2560,128]{0,1:T(8,128)}, f32[2560,128]{1,0:T(8,128)})) %all-reduce.7.cloned.1.call-update) | async-done | bytes 2621456 | tf_op jit(solution)/shard_map/psum | solution.py:249
  502.6 9.3 %fusion.52 = f32[2,40,64,64]{3,2,1,0:T(8,128)} fusion(f32[2,64,40,64]{1,3,2,0:T(8,128)} %copy.93, f32[2,64,40,64]{1,3,2,0:T(8,128)S(1)} %copy.89, f32[2,40,64]{2,1,0:T(8,128)S(1)} %get-tuple-element.498, f32[2,64,40,64]{1,3,2,0:T(8,128)} %copy.91, f32[2,64,40,64]{1,3,2,0:T(8,128)} %copy.90), kind=kOutput, calls=%fused_computation.86 | convolution fusion | flops 253296640 | bytes 6574080 | tf_op jit(solution)/shard_map/nthk,nshk->nhts/dot_general | solution.py:29
  511.9 58.1 %all-reduce = (f32[2560]{0:T(1024)S(1)}, f32[2560]{0:T(1024)S(1)}) all-reduce(f32[2560]{0:T(1024)S(1)} %get-tuple-element.496, f32[2560]{0:T(1024)S(1)} %multiply_reduce_fusion.2), channel_id=1, replica_groups=mesh['seq'=16,'dp'=2] {'seq'}, use_global_device_ids=true, to_apply=%region_18.19 | all-reduce | flops 5120 | bytes 40960 | tf_op jit(solution)/shard_map/psum | solution.py:249
  570.0 20.6 %all-reduce.2 = (f32[2560]{0:T(1024)S(1)}, f32[2560]{0:T(1024)S(1)}) all-reduce(f32[2560]{0:T(1024)S(1)} %get-tuple-element.475, f32[2560]{0:T(1024)S(1)} %get-tuple-element.476), channel_id=1, replica_groups=mesh['seq'=16,'dp'=2] {'dp'}, use_global_device_ids=true, to_apply=%region_19.20 | all-reduce | flops 5120 | bytes 40960 | tf_op jit(solution)/shard_map/psum | solution.py:249
  592.0 8.3 %fusion.23 = f32[2,40,64,64]{2,3,1,0:T(8,128)S(1)} fusion(f32[2,40,64,64]{2,3,1,0:T(8,128)} %get-tuple-element.330, f32[40,64,64]{1,2,0:T(8,128)} %copy.119, f32[2,40,64]{2,1,0:T(8,128)S(1)} %copy-done.22, f32[2,64,40,64]{1,3,2,0:T(8,128)} %copy.93, f32[2,64,40,64]{1,3,2,0:T(8,128)S(1)} %copy.89, f32[2,40,64]{2,1,0:T(8,128)S(1)} %copy-done.20), kind=kOutput, calls=%fused_computation.63 | convolution fusion | flops 252968960 | bytes 5939200 | tf_op jit(solution)/shard_map/nthk,nhkv->nthv/dot_general | solution.py:29
  600.3 3.0 fusion.7
  605.2 2.8 convert_element_type.122
  608.0 8.7 %fusion.22 = f32[2,40,64,64]{2,3,1,0:T(8,128)S(1)} fusion(f32[2,40,64,64]{2,3,1,0:T(8,128)} %get-tuple-element.325, f32[40,64,64]{1,2,0:T(8,128)} %copy.103, f32[2,40,64]{2,1,0:T(8,128)S(1)} %get-tuple-element.321, f32[2,64,40,64]{1,3,2,0:T(8,128)} %copy.91, f32[2,64,40,64]{1,3,2,0:T(8,128)S(1)} %copy.89, f32[2,64,40,64]{1,3,2,0:T(8,128)} %copy.90), kind=kOutput, calls=%fused_computation.62 | convolution fusion | flops 252968960 | bytes 7229440 | tf_op jit(solution)/shard_map/nthk,nhkv->nthv/dot_general | solution.py:29
  (137 shorter events, 80.5 us)
Async XLA Ops:
  7.2 2.4 copy-start
  7.2 164.0 %all-gather.7.cloned.1.call-start = ((), (), s32[]{:S(2)}) async-start(), calls=%async_computation | async-start | bytes 22282240 | tf_op jit(solution)/shard_map/all_gather | solution.py:16
  12.8 1.5 copy-start.12
  19.0 9.6 %copy-start.19 = (f32[2,40,64]{2,1,0:T(8,128)}, f32[2,40,64]{2,1,0:T(8,128)S(1)}, u32[]{:S(2)}) copy-start(f32[2,40,64]{2,1,0:T(8,128)S(1)} %get-tuple-element.499) | copy-start | bytes 61444
  53.7 228.2 %all-gather.9.cloned.1.call-start = ((), (), s32[]{:S(2)}) async-start(), calls=%async_computation.1 | async-start | bytes 22282240 | tf_op jit(solution)/shard_map/all_gather | solution.py:16
  105.4 397.2 %all-reduce.7.cloned.1.call-start = ((), (), s32[]{:S(2)}) async-start(), calls=%async_computation.2 | async-start | bytes 5242880 | tf_op jit(solution)/shard_map/psum | solution.py:249
  106.2 53.0 %copy-start.5 = (bf16[2,64,40,64]{3,2,1,0:T(8,128)(2,1)S(1)}, bf16[2,64,40,64]{3,2,1,0:T(8,128)(2,1)}, u32[]{:S(2)}) copy-start(bf16[2,64,40,64]{3,2,1,0:T(8,128)(2,1)} %reshape.124) | copy-start | bytes 1966084
  106.2 53.0 %copy-start.7 = (bf16[2,64,40,64]{3,2,1,0:T(8,128)(2,1)S(1)}, bf16[2,64,40,64]{3,2,1,0:T(8,128)(2,1)}, u32[]{:S(2)}) copy-start(bf16[2,64,40,64]{3,2,1,0:T(8,128)(2,1)} %reshape.125) | copy-start | bytes 1966084
  343.3 2.8 copy-start.21
  346.1 6.5 %copy-start.4 = (f32[2,40,64,64]{2,3,1,0:T(8,128)S(1)}, f32[2,40,64,64]{2,3,1,0:T(8,128)}, u32[]{:S(2)}) copy-start(f32[2,40,64,64]{2,3,1,0:T(8,128)} %get-tuple-element.781) | copy-start | bytes 3932164
  346.1 6.5 %copy-start.10 = (f32[2,40,64,64]{2,3,1,0:T(8,128)S(1)}, f32[2,40,64,64]{2,3,1,0:T(8,128)}, u32[]{:S(2)}) copy-start(f32[2,40,64,64]{2,3,1,0:T(8,128)} %get-tuple-element.325) | copy-start | bytes 3932164
  346.1 6.5 %copy-start.11 = (f32[2,40,64,64]{2,3,1,0:T(8,128)S(1)}, f32[2,40,64,64]{2,3,1,0:T(8,128)}, u32[]{:S(2)}) copy-start(f32[2,40,64,64]{2,3,1,0:T(8,128)} %get-tuple-element.330) | copy-start | bytes 3932164
  352.6 4.1 copy-start.8
  352.6 4.1 copy-start.16
  356.7 2.4 copy-start.1
  356.7 2.5 copy-start.2
  356.7 3.3 copy-start.15
  360.0 6.8 %copy-start.3 = (f32[2,64,40,64]{1,3,2,0:T(8,128)S(1)}, f32[2,64,40,64]{1,3,2,0:T(8,128)}, u32[]{:S(2)}) copy-start(f32[2,64,40,64]{1,3,2,0:T(8,128)} %copy.91) | copy-start | bytes 3932164
  360.0 6.8 %copy-start.20 = (f32[2,40,64]{2,1,0:T(8,128)S(1)}, f32[2,40,64]{2,1,0:T(8,128)}, u32[]{:S(2)}) copy-start(f32[2,40,64]{2,1,0:T(8,128)} %copy-done.19) | copy-start | bytes 61444
  360.0 6.8 %copy-start.23 = (f32[2,64,40]{1,2,0:T(8,128)S(1)}, f32[2,64,40]{1,2,0:T(8,128)}, u32[]{:S(2)}) copy-start(f32[2,64,40]{1,2,0:T(8,128)} %fusion.5) | copy-start | bytes 61444
  398.7 4.3 copy-start.18
  402.4 0.6 copy-start.26
  404.5 225.6 %all-reduce.9.cloned.1.call-start = ((), (), s32[]{:S(2)}) async-start(), calls=%async_computation.3 | async-start | bytes 5242880 | tf_op jit(solution)/shard_map/psum | solution.py:249
  502.6 89.4 %copy-start.22 = (f32[2,40,64]{2,1,0:T(8,128)S(1)}, f32[2,40,64]{2,1,0:T(8,128)}, u32[]{:S(2)}) copy-start(f32[2,40,64]{2,1,0:T(8,128)} %get-tuple-element.326) | copy-start | bytes 61444
  592.0 8.3 %copy-start.9 = (bf16[2,64,40,64]{3,2,1,0:T(8,128)(2,1)S(1)}, bf16[2,64,40,64]{3,2,1,0:T(8,128)(2,1)}, u32[]{:S(2)}) copy-start(bf16[2,64,40,64]{3,2,1,0:T(8,128)(2,1)} %reshape.125) | copy-start | bytes 1966084
  592.0 8.3 %copy-start.13 = (f32[2,40,64,64]{3,2,1,0:T(8,128)S(1)}, f32[2,40,64,64]{3,2,1,0:T(8,128)}, u32[]{:S(2)}) copy-start(f32[2,40,64,64]{3,2,1,0:T(8,128)} %fusion.52) | copy-start | bytes 3932164
  592.0 8.3 %copy-start.24 = (f32[2,64,40]{1,2,0:T(8,128)S(1)}, f32[2,64,40]{1,2,0:T(8,128)}, u32[]{:S(2)}) copy-start(f32[2,64,40]{1,2,0:T(8,128)} %get-tuple-element.495) | copy-start | bytes 61444
  608.0 8.7 %copy-start.6 = (bf16[2,64,40,64]{3,2,1,0:T(8,128)(2,1)S(1)}, bf16[2,64,40,64]{3,2,1,0:T(8,128)(2,1)}, u32[]{:S(2)}) copy-start(bf16[2,64,40,64]{3,2,1,0:T(8,128)(2,1)} %reshape.124) | copy-start | bytes 1966084
  608.0 8.7 %copy-start.14 = (f32[2,40,64,64]{3,2,1,0:T(8,128)S(1)}, f32[2,40,64,64]{3,2,1,0:T(8,128)}, u32[]{:S(2)}) copy-start(f32[2,40,64,64]{3,2,1,0:T(8,128)} %fusion.52) | copy-start | bytes 3932164
  621.6 3.8 copy-start.17
  625.4 2.5 copy-start.27
  630.1 2.3 copy-start.25
Sparse Core Ops, SparseCore 0:
  53.8 117.4 all-gather.6
  172.8 108.9 all-gather.8
  404.7 97.8 all-reduce.6
  504.8 74.4 all-reduce.8
